TPU v7x, 32 devices: a whole 2x2x4 slice. The times are simulated.
32 devices in a mesh: batch: 4 (over x, core), lat: 8 (over z, y).
Axes of the slice: x: 2, y: 2, z: 4, core: 2. Of those that a mesh axis runs over, the one named last changes fastest.
Arguments:
- predicted: bfloat16 [4, 73, 192, 1440], P('batch', None, 'lat'), may hold values from -64 to 64
- target: bfloat16 [4, 73, 192, 1440], P('batch', None, 'lat'), may hold values from -128 to 128
- legendre_basis: bfloat16 [192, 96, 720], P(None, ('batch', 'lat')), may hold values from -1 to 1
Outputs:
- spectra: float32 [2, 73, 720], replicated
- channel_loss: float32 [73], replicated
All inputs are finite; a program needn't handle non-finite values.
Results may differ from a plain program's by a relative error of at most 0.0003.
Values may be sent and summed in bfloat16 or wider, within the bound.
No kernel may reach another device: no remote copies, remote signals or barrier semaphores. Data moves between devices by JAX's collectives and lax.ppermute only.
A program may use at most 128 MiB of HBM per device.

v0:
```python
import math
import jax
import jax.numpy as jnp
from jax import lax
from jax.sharding import PartitionSpec as P


def fourier_table(lon_count, order_count):
    lon_ids = jnp.arange(lon_count, dtype=jnp.int32)
    order_ids = jnp.arange(order_count, dtype=jnp.int32)
    product_ids = lon_ids[:, None] * order_ids[None, :] % lon_count
    angles = 2.0 * math.pi / lon_count * product_ids.astype(jnp.float32)
    inv_root = 1.0 / math.sqrt(lon_count)
    return jnp.stack([jnp.cos(angles) * inv_root, -jnp.sin(angles) * inv_root], axis=1).astype(
        jnp.bfloat16
    )


def band_energy(fourier, basis_block, orders):
    coefficients = jnp.einsum(
        "fpmbcn,nml->fpmbcl", fourier, basis_block, preferred_element_type=jnp.float32
    )
    squares = jnp.sum(coefficients * coefficients, axis=1)
    weights = jnp.where(orders == 0, 1.0, 2.0).astype(jnp.float32)
    return jnp.sum(squares * weights[None, :, None, None, None], axis=(1, 2))


def body(predicted, target, legendre_basis):
    groups = lax.axis_size("batch")
    band_count = lax.axis_size("lat")
    per_dev = legendre_basis.shape[1]
    order_count = per_dev * groups * band_count
    dft_table = fourier_table(predicted.shape[3], order_count)
    band_id = lax.axis_index("lat")

    def transform(field_in):
        return jnp.einsum(
            "bcnk,kpm->pmbcn", field_in, dft_table, preferred_element_type=jnp.float32
        ).astype(jnp.bfloat16)

    fourier = jnp.stack([transform(predicted), transform(target)], axis=0)
    members = fourier.shape[3]
    channels = fourier.shape[4]
    lat_rows = fourier.shape[5]
    fourier = fourier.reshape(2, 2, groups, band_count, per_dev, members, channels, lat_rows)
    arrived = lax.all_to_all(fourier, "lat", split_axis=3, concat_axis=7, tiled=True)
    arrived = arrived.reshape(
        2, 2, groups * per_dev, arrived.shape[5], arrived.shape[6], arrived.shape[7]
    )
    basis_block = lax.all_gather(legendre_basis, "batch", axis=1, tiled=True)
    taken = basis_block.shape[1]
    gathered_ids = jnp.arange(taken, dtype=jnp.int32)
    orders = (
        gathered_ids // per_dev * band_count * per_dev + band_id * per_dev + gathered_ids % per_dev
    )
    partial_value = band_energy(arrived, basis_block, orders)
    energy = lax.psum(partial_value, "lat")
    energy = lax.psum(energy, "batch")
    spectra = energy / (predicted.shape[0] * groups * order_count)
    log_spectra = jnp.log(spectra + 1e-06)
    channel_loss = jnp.mean((log_spectra[0] - log_spectra[1]) ** 2, axis=1)
    return (spectra, channel_loss)


def solution(mesh):
    placed = (
        P("batch", None, "lat", None),
        P("batch", None, "lat", None),
        P(None, ("batch", "lat"), None),
    )
    return jax.shard_map(body, mesh=mesh, in_specs=placed, out_specs=(P(), P()), check_vma=False)
```

profile of v0, /device:TPU:0, one launch (start us, length us, event | category | flops | bytes accessed | tf_op | source)
XLA Modules:
  0.0 212.2 jit_solution(11625327290755649896)
XLA Ops:
  7.2 0.0 all-gather.2.cloned.1.call-start
  7.2 0.7 all-gather.2.cloned.1.call-update
  7.9 2.6 %multiply_convert_fusion = (bf16[1440,1,96]{0,2,1:T(8,128)(2,1)S(1)}, bf16[1440,1,96]{0,2,1:T(8,128)(2,1)S(1)}) fusion(), kind=kLoop, calls=%fused_computation.17 | loop fusion | flops 1935360 | bytes 552960 | tf_op jit(solution)/shard_map/convert.1
  10.5 0.0 copy-start
  10.5 0.0 copy-start.1
  10.5 0.7 copy-done
  11.2 0.1 copy-done.1
  11.3 4.8 %fusion.8 = bf16[2,96,73,24]{1,2,3,0:T(8,128)(2,1)S(1)} fusion(bf16[73,24,1440]{2,1,0:T(8,128)(2,1)} %bitcast.33, bf16[1440,1,96]{0,2,1:T(8,128)(2,1)S(1)} %get-tuple-element.4, bf16[1440,1,96]{0,2,1:T(8,128)(2,1)S(1)} %get-tuple-element.5), kind=kOutput, calls=%fused_computation.11 | convolution fusion | flops 970228224 | bytes 6271488 | tf_op jit(solution)/shard_map/bcnk,kpm->pmbcn/dot_general | solution.py:37
  16.1 0.9 copy.29
  17.0 5.5 %fusion.11 = bf16[2,96,73,24]{1,2,3,0:T(8,128)(2,1)S(1)} fusion(bf16[73,24,1440]{2,1,0:T(8,128)(2,1)} %bitcast.34, bf16[1440,1,96]{0,2,1:T(8,128)(2,1)} %copy-done, bf16[1440,1,96]{0,2,1:T(8,128)(2,1)} %copy-done.1), kind=kOutput, calls=%fused_computation.12 | convolution fusion | flops 970228224 | bytes 6271488 | tf_op jit(solution)/shard_map/bcnk,kpm->pmbcn/dot_general | solution.py:37
  22.5 0.9 copy.31
  23.3 0.5 pad_maximum_fusion
  23.9 2.0 copy.32
  25.9 7.5 %all-to-all-start = ((bf16[2,2,4,8,3,1,73,24]{6,7,4,2,1,5,0,3:T(8,128)(2,1)}), bf16[2,2,4,8,3,1,73,24]{6,7,4,2,1,5,0,3:T(8,128)(2,1)S(1)}, u32[]{:S(2)}, u32[]{:S(2)}) async-start(bf16[2,2,4,8,3,1,73,24]{6,7,4,2,1,5,0,3:T(8,128)(2,1)} %copy.32), calls=%async_computation | async-start | bytes 4718592 | tf_op jit(solution)/shard_map/all_to_all | solution.py:46
  33.5 0.0 all-reduce.3.cloned.1.call-start
  33.5 53.6 %all-to-all-done = bf16[2,2,4,8,3,1,73,24]{6,7,4,2,1,5,0,3:T(8,128)(2,1)S(1)} async-done(((bf16[2,2,4,8,3,1,73,24]{6,7,4,2,1,5,0,3:T(8,128)(2,1)}), bf16[2,2,4,8,3,1,73,24]{6,7,4,2,1,5,0,3:T(8,128)(2,1)S(1)}, u32[]{:S(2)}, u32[]{:S(2)}) %all-to-all-start) | async-done | bytes 1345568 | tf_op jit(solution)/shard_map/all_to_all | solution.py:46
  87.1 2.1 copy.33
  89.2 0.0 all-gather.2.cloned.1.call-done
  89.2 5.1 %multiply_reduce_fusion = f32[12,2,73,720]{3,2,1,0:T(8,128)S(1)} fusion(bf16[192,12,720]{2,0,1:T(8,128)(2,1)} %all-gather.2.cloned.1.call-done, bf16[2,2,12,73,192]{3,4,2,1,0:T(8,128)(2,1)} %bitcast.30), kind=kOutput, calls=%fused_computation | convolution fusion | flops 972570240 | bytes 9709056 | tf_op jit(solution)/shard_map/fpmbcn,nml->fpmbcl/dot_general | solution.py:20
  94.3 0.6 multiply_reduce_fusion.1
  94.9 1.1 copy.40
  96.0 0.0 all-reduce.3.cloned.1.call-update
  96.1 0.0 all-reduce.5.cloned.1.call-start
  96.1 71.4 %all-reduce.3.cloned.1.call-done = f32[2,73,720]{2,0,1:T(2,128)} async-done(((f32[2,73,720]{2,0,1:T(2,128)}), f32[2,73,720]{2,0,1:T(2,128)}) %all-reduce.3.cloned.1.call-update) | async-done | bytes 420496 | tf_op jit(solution)/shard_map/psum | solution.py:57
  167.5 0.0 all-reduce.5.cloned.1.call-update
  167.6 34.7 %all-reduce.5.cloned.1.call-done = f32[2,73,720]{2,0,1:T(2,128)} async-done(((f32[2,73,720]{2,0,1:T(2,128)}), f32[2,73,720]{2,0,1:T(2,128)}) %all-reduce.5.cloned.1.call-update) | async-done | bytes 420496 | tf_op jit(solution)/shard_map/psum | solution.py:58
  202.2 2.2 %add_log_fusion = (f32[2,73,720]{2,0,1:T(2,128)S(1)}, f32[2,73,720]{2,0,1:T(2,128)}) fusion(f32[2,73,720]{2,0,1:T(2,128)} %all-reduce.5.cloned.1.call-done), kind=kLoop, calls=%fused_computation.23 | loop fusion | flops 210240 | bytes 1261440 | tf_op jit(solution)/shard_map/log | solution.py:60
  204.5 0.6 fusion.20
  205.1 0.5 broadcast_multiply_fusion.1
  (1 shorter events, 0.0 us)
Async XLA Ops:
  7.2 82.1 %all-gather.2.cloned.1.call-start = ((), (), s32[]{:S(2)}) async-start(), calls=%async_computation.1 | async-start | bytes 4423680 | tf_op jit(solution)/shard_map/all_gather | solution.py:50
  10.5 0.7 copy-start
  10.5 0.8 copy-start.1
  25.9 61.2 %all-to-all-start = ((bf16[2,2,4,8,3,1,73,24]{6,7,4,2,1,5,0,3:T(8,128)(2,1)}), bf16[2,2,4,8,3,1,73,24]{6,7,4,2,1,5,0,3:T(8,128)(2,1)S(1)}, u32[]{:S(2)}, u32[]{:S(2)}) async-start(bf16[2,2,4,8,3,1,73,24]{6,7,4,2,1,5,0,3:T(8,128)(2,1)} %copy.32), calls=%async_computation | async-start | bytes 4718592 | tf_op jit(solution)/shard_map/all_to_all | solution.py:46
  33.5 134.1 %all-reduce.3.cloned.1.call-start = ((), (), s32[]{:S(2)}) async-start(), calls=%async_computation.2 | async-start | bytes 897024 | tf_op jit(solution)/shard_map/psum | solution.py:57
  96.1 106.2 %all-reduce.5.cloned.1.call-start = ((), (), s32[]{:S(2)}) async-start(), calls=%async_computation.3 | async-start | bytes 897024 | tf_op jit(solution)/shard_map/psum | solution.py:58
Sparse Core Ops, SparseCore 0:
  9.5 33.4 all-gather.1
  96.2 71.2 all-reduce.2
  169.9 32.2 all-reduce.4
where the time goes:
time: 212 us
  waiting for transfers between devices  160 us (75%)
  matrix products  15.4 us (7%)
  between operations  13.8 us (7%)
  local copies, waits for them, and re-layouts  7.77 us (4%)
  starting transfers between devices  7.66 us (4%)
  other arithmetic  7.07 us (3%)
    psum x1, waiting for transfers between devices, body(): energy = lax.psum(partial_value, 'lat')  71.4 us
    all_to_all x1, waiting for transfers between devices, body(): lax.all_to_all(fourier, 'lat', split_axis=3, concat_axis=7, tiled=True)  53.6 us
    psum x1, waiting for transfers between devices, body(): energy = lax.psum(energy, 'batch')  34.7 us
    dot_general x2, matrix products, transform(): jnp.einsum('bcnk,kpm->pmbcn', field_in, dft_table, preferred_element_type...  10.3 us
    all_to_all x1, starting transfers between devices, body(): lax.all_to_all(fourier, 'lat', split_axis=3, concat_axis=7, tiled=True)  7.55 us
    dot_general x1, matrix products, band_energy(): jnp.einsum('fpmbcn,nml->fpmbcl', fourier, basis_block, preferred_element_...  5.1 us
  transfers between devices with their start and end apart: 4, of which 3 were waited for; matrix products, arithmetic and copies ran while one was open for 9% of the time, Pallas kernels for 0%

commit v1 on v0

--- a/solution.py
+++ b/solution.py
@@ -55,7 +55,9 @@
     )
     partial_value = band_energy(arrived, basis_block, orders)
     energy = lax.psum(partial_value, "lat")
-    energy = lax.psum(energy, "batch")
+    energy = energy
+    for hop in (1, 2):
+        energy = energy + lax.ppermute(energy, "batch", [(dev, dev ^ hop) for dev in range(4)])
     spectra = energy / (predicted.shape[0] * groups * order_count)
     log_spectra = jnp.log(spectra + 1e-06)
     channel_loss = jnp.mean((log_spectra[0] - log_spectra[1]) ** 2, axis=1)

time: 212 us -> 193 us (0.910)
  waiting for transfers between devices: 160 us -> 138 us
    psum x1 -> x0, waiting for transfers between devices: 34.7 us -> none  [body(): energy = lax.psum(energy, 'batch')]
    ppermute x0 -> x2, waiting for transfers between devices: none -> 12.9 us  [body(): lax.ppermute(energy, 'batch', [(dev, dev ^ hop) for dev in range(4)])]
  transfers between devices with their start and end apart: 4 -> 5, of which waited for: 3 -> 4; matrix products, arithmetic and copies ran while one was open for 9% -> 10% of each run, Pallas kernels for 0% -> 0%
where the time goes in v1:
time: 193 us; the launch traced here: 192 us
  waiting for transfers between devices  138 us (72%)
  matrix products  15.4 us (8%)
  between operations  14.1 us (7%)
  starting transfers between devices  9.33 us (5%)
  local copies, waits for them, and re-layouts  7.75 us (4%)
  other arithmetic  7.38 us (4%)
    psum x1, waiting for transfers between devices, body(): energy = lax.psum(partial_value, 'lat')  71.5 us
    all_to_all x1, waiting for transfers between devices, body(): lax.all_to_all(fourier, 'lat', split_axis=3, concat_axis=7, tiled=True)  53.4 us
    ppermute x2, waiting for transfers between devices, body(): lax.ppermute(energy, 'batch', [(dev, dev ^ hop) for dev in range(4)])  12.9 us
    dot_general x2, matrix products, transform(): jnp.einsum('bcnk,kpm->pmbcn', field_in, dft_table, preferred_element_type...  10.3 us
    all_to_all x1, starting transfers between devices, body(): lax.all_to_all(fourier, 'lat', split_axis=3, concat_axis=7, tiled=True)  7.54 us
    dot_general x1, matrix products, band_energy(): jnp.einsum('fpmbcn,nml->fpmbcl', fourier, basis_block, preferred_element_...  5.1 us
  transfers between devices with their start and end apart: 5, of which 4 were waited for; matrix products, arithmetic and copies ran while one was open for 10% of the time, Pallas kernels for 0%

profile of v1, /device:TPU:0, one launch (start us, length us, event | category | flops | bytes accessed | tf_op | source)
XLA Modules:
  0.0 192.5 jit_solution(503882210114959273)
XLA Ops:
  7.2 0.0 all-gather.2.cloned.1.call-start
  7.2 0.7 all-gather.2.cloned.1.call-update
  7.9 2.6 %multiply_convert_fusion = (bf16[1440,1,96]{0,2,1:T(8,128)(2,1)S(1)}, bf16[1440,1,96]{0,2,1:T(8,128)(2,1)S(1)}) fusion(), kind=kLoop, calls=%fused_computation.17 | loop fusion | flops 1935360 | bytes 552960 | tf_op jit(solution)/shard_map/convert.1
  10.5 0.0 copy-start
  10.5 0.0 copy-start.1
  10.5 0.7 copy-done
  11.2 0.1 copy-done.1
  11.3 4.8 %fusion.8 = bf16[2,96,73,24]{1,2,3,0:T(8,128)(2,1)S(1)} fusion(bf16[73,24,1440]{2,1,0:T(8,128)(2,1)} %bitcast.33, bf16[1440,1,96]{0,2,1:T(8,128)(2,1)S(1)} %get-tuple-element.4, bf16[1440,1,96]{0,2,1:T(8,128)(2,1)S(1)} %get-tuple-element.5), kind=kOutput, calls=%fused_computation.11 | convolution fusion | flops 970228224 | bytes 6271488 | tf_op jit(solution)/shard_map/bcnk,kpm->pmbcn/dot_general | solution.py:37
  16.1 0.9 copy.29
  17.0 5.5 %fusion.11 = bf16[2,96,73,24]{1,2,3,0:T(8,128)(2,1)S(1)} fusion(bf16[73,24,1440]{2,1,0:T(8,128)(2,1)} %bitcast.34, bf16[1440,1,96]{0,2,1:T(8,128)(2,1)} %copy-done, bf16[1440,1,96]{0,2,1:T(8,128)(2,1)} %copy-done.1), kind=kOutput, calls=%fused_computation.12 | convolution fusion | flops 970228224 | bytes 6271488 | tf_op jit(solution)/shard_map/bcnk,kpm->pmbcn/dot_general | solution.py:37
  22.5 0.9 copy.31
  23.4 0.5 pad_maximum_fusion
  23.9 2.0 %copy.32 = bf16[2,2,4,8,3,1,73,24]{6,7,4,2,1,5,0,3:T(8,128)(2,1)} copy(bf16[2,2,4,8,3,1,73,24]{6,7,4,3,2,1,5,0:T(8,128)(2,1)S(1)} %pad_maximum_fusion) | data formatting | bytes 2691072 | tf_op jit(solution)/shard_map/stack | solution.py:41
  25.9 7.5 %all-to-all-start = ((bf16[2,2,4,8,3,1,73,24]{6,7,4,2,1,5,0,3:T(8,128)(2,1)}), bf16[2,2,4,8,3,1,73,24]{6,7,4,2,1,5,0,3:T(8,128)(2,1)S(1)}, u32[]{:S(2)}, u32[]{:S(2)}) async-start(bf16[2,2,4,8,3,1,73,24]{6,7,4,2,1,5,0,3:T(8,128)(2,1)} %copy.32), calls=%async_computation | async-start | bytes 4718592 | tf_op jit(solution)/shard_map/all_to_all | solution.py:46
  33.5 0.2 all-reduce.2.cloned.1.call-start
  33.7 53.4 %all-to-all-done = bf16[2,2,4,8,3,1,73,24]{6,7,4,2,1,5,0,3:T(8,128)(2,1)S(1)} async-done(((bf16[2,2,4,8,3,1,73,24]{6,7,4,2,1,5,0,3:T(8,128)(2,1)}), bf16[2,2,4,8,3,1,73,24]{6,7,4,2,1,5,0,3:T(8,128)(2,1)S(1)}, u32[]{:S(2)}, u32[]{:S(2)}) %all-to-all-start) | async-done | bytes 1345568 | tf_op jit(solution)/shard_map/all_to_all | solution.py:46
  87.1 2.1 %copy.33 = bf16[2,2,4,1,3,1,73,8,24]{6,8,7,4,2,1,0,5,3:T(8,128)(2,1)} copy(bf16[2,2,4,1,3,1,73,8,24]{6,8,4,2,1,0,7,5,3:T(8,128)(2,1)S(1)} %bitcast.29) | data formatting | bytes 2691072 | tf_op jit(solution)/shard_map/all_to_all | solution.py:46
  89.2 0.0 all-gather.2.cloned.1.call-done
  89.2 5.1 %multiply_reduce_fusion = f32[12,2,73,720]{3,2,1,0:T(8,128)S(1)} fusion(bf16[192,12,720]{2,0,1:T(8,128)(2,1)} %all-gather.2.cloned.1.call-done, bf16[2,2,12,73,192]{3,4,2,1,0:T(8,128)(2,1)} %bitcast.30), kind=kOutput, calls=%fused_computation | convolution fusion | flops 972570240 | bytes 9709056 | tf_op jit(solution)/shard_map/fpmbcn,nml->fpmbcl/dot_general | solution.py:20
  94.3 0.6 multiply_reduce_fusion.1
  94.9 1.1 copy.40
  96.0 0.0 all-reduce.2.cloned.1.call-update
  96.0 71.5 %all-reduce.2.cloned.1.call-done = f32[2,73,720]{2,0,1:T(2,128)} async-done(((f32[2,73,720]{2,0,1:T(2,128)}), f32[2,73,720]{2,0,1:T(2,128)}) %all-reduce.2.cloned.1.call-update) | async-done | bytes 420496 | tf_op jit(solution)/shard_map/psum | solution.py:57
  167.5 0.0 collective-permute-start
  167.5 2.0 %collective-permute-done = f32[2,73,720]{2,0,1:T(2,128)S(1)} collective-permute-done((f32[2,73,720]{2,0,1:T(2,128)}, f32[2,73,720]{2,0,1:T(2,128)S(1)}, u32[]{:S(2)}, u32[]{:S(2)}) %collective-permute-start) | collective-permute-done | bytes 420512 | tf_op jit(solution)/shard_map/ppermute | solution.py:60
  169.5 1.2 add.70
  170.8 1.5 collective-permute-start.1
  172.3 10.9 %collective-permute-done.1 = f32[2,73,720]{2,0,1:T(2,128)S(1)} collective-permute-done((f32[2,73,720]{2,0,1:T(2,128)S(1)}, f32[2,73,720]{2,0,1:T(2,128)S(1)}, u32[]{:S(2)}, u32[]{:S(2)}) %collective-permute-start.1) | collective-permute-done | bytes 420512 | tf_op jit(solution)/shard_map/ppermute | solution.py:60
  183.2 1.3 add_log_fusion
  184.5 0.6 fusion.20
  185.1 0.5 broadcast_multiply_fusion
  (1 shorter events, 0.0 us)
Async XLA Ops:
  7.2 82.1 %all-gather.2.cloned.1.call-start = ((), (), s32[]{:S(2)}) async-start(), calls=%async_computation.1 | async-start | bytes 4423680 | tf_op jit(solution)/shard_map/all_gather | solution.py:50
  10.5 0.7 copy-start
  10.5 0.8 copy-start.1
  25.9 61.2 %all-to-all-start = ((bf16[2,2,4,8,3,1,73,24]{6,7,4,2,1,5,0,3:T(8,128)(2,1)}), bf16[2,2,4,8,3,1,73,24]{6,7,4,2,1,5,0,3:T(8,128)(2,1)S(1)}, u32[]{:S(2)}, u32[]{:S(2)}) async-start(bf16[2,2,4,8,3,1,73,24]{6,7,4,2,1,5,0,3:T(8,128)(2,1)} %copy.32), calls=%async_computation | async-start | bytes 4718592 | tf_op jit(solution)/shard_map/all_to_all | solution.py:46
  33.5 134.1 %all-reduce.2.cloned.1.call-start = ((), (), s32[]{:S(2)}) async-start(), calls=%async_computation.2 | async-start | bytes 897024 | tf_op jit(solution)/shard_map/psum | solution.py:57
  167.5 2.0 %collective-permute-start = (f32[2,73,720]{2,0,1:T(2,128)}, f32[2,73,720]{2,0,1:T(2,128)S(1)}, u32[]{:S(2)}, u32[]{:S(2)}) collective-permute-start(f32[2,73,720]{2,0,1:T(2,128)} %all-reduce.2.cloned.1.call-done), channel_id=1, source_target_pairs={{0,8},{8,0},{16,24},{24,16},{1,9},{9,1},{17,25},{25,17},{2,10},{10... | collective-permute-start | bytes 1261448 | tf_op jit(solution)/shard_map/ppermute | solution.py:60
  170.8 12.4 %collective-permute-start.1 = (f32[2,73,720]{2,0,1:T(2,128)S(1)}, f32[2,73,720]{2,0,1:T(2,128)S(1)}, u32[]{:S(2)}, u32[]{:S(2)}) collective-permute-start(f32[2,73,720]{2,0,1:T(2,128)S(1)} %add.70), channel_id=1, source_target_pairs={{0,16},{8,24},{16,0},{24,8},{1,17},{9,25},{17,1},{25,9},{2,18},{10... | collective-permute-start | bytes 1261448 | tf_op jit(solution)/shard_map/ppermute | solution.py:60
Sparse Core Ops, SparseCore 0:
  9.5 33.4 all-gather.1
  96.2 71.3 all-reduce.1
